TPU v7x, 32 devices: a whole 2x2x4 slice. The times are simulated.
32 devices in a mesh: expert: 4 (over x, core), rows: 8 (over z, y).
Axes of the slice: x: 2, y: 2, z: 4, core: 2. Of those that a mesh axis runs over, the one named last changes fastest.
Arguments:
- step: int32 [], replicated, may hold values from 2 to 8
- gradient: bfloat16 [4, 4096, 14336], P('expert', 'rows'), may hold values from -8 to 8
- weight: bfloat16 [4, 4096, 14336], P('expert', 'rows'), may hold values from -0.119628906 to 0.119628906
- row_state: float32 [4, 4096], P('expert', 'rows'), may hold values from 0.3 to 3
- col_state: float32 [4, 14336], P('expert', 'rows'), may hold values from 0.3 to 3
- prev_msq: float32 [4, 8], P('expert', 'rows'), may hold values from 2 to 500
Outputs:
- new_weight: bfloat16 [4, 4096, 14336], P('expert', 'rows')
- new_row_state: float32 [4, 4096], P('expert', 'rows')
- new_col_state: float32 [4, 14336], P('expert', 'rows')
- new_msq: float32 [4, 8], P('expert', 'rows')
All inputs are finite; a program needn't handle non-finite values.
Results may differ from a plain program's by a relative error of at most 0.001.
Values sent between devices are 32-bit elements; how exact they have to be, the bound alone decides.
A program may use at most 128 MiB of HBM per device.

v0:
```python
import jax
import jax.numpy as jnp
from jax import lax
from jax.sharding import PartitionSpec as P


def shards(step, gradient, weight, row_state, col_state, prev_msq):
    local_experts = gradient.shape[0]
    local_rows = gradient.shape[1]
    columns = gradient.shape[2]
    row_devices = lax.axis_size("rows")
    expert_devices = lax.axis_size("expert")
    all_rows = local_rows * row_devices
    beta = 1.0 - step.astype(jnp.float32) ** (-0.8)
    grad = gradient.astype(jnp.float32)
    squares = grad * grad + 1e-30
    new_row = beta * row_state + (1.0 - beta) * jnp.mean(squares, axis=2)
    partial_cols = jnp.sum(squares, axis=1)
    clip_term = jnp.sum(prev_msq)
    row_sum = jnp.sum(new_row, axis=1)
    clip_total = lax.psum(clip_term, ("expert", "rows"))
    row_totals = lax.psum(row_sum, "rows")
    entries = prev_msq.shape[0] * prev_msq.shape[1] * expert_devices * row_devices
    clip = jnp.sqrt(clip_total / entries)
    row_mean = row_totals / all_rows
    old_full = lax.all_gather(col_state, "rows", axis=1, tiled=True)
    col_totals = lax.psum(partial_cols, "rows")
    full_cols = beta * old_full + (1.0 - beta) * col_totals / all_rows
    width = columns // row_devices
    new_col = lax.dynamic_slice_in_dim(full_cols, lax.axis_index("rows") * width, width, 1)
    scaled = new_row[:, :, None] * full_cols[:, None, :] / row_mean[:, None, None]
    update = grad / jnp.sqrt(scaled) / clip
    new_weight = (weight.astype(jnp.float32) - 0.01 * update).astype(jnp.bfloat16)
    new_msq = jnp.mean(update * update, axis=(1, 2)).reshape(local_experts, 1)
    return (new_weight, new_row, new_col, new_msq)


def solution(mesh):
    placed = (
        P(),
        P("expert", "rows", None),
        P("expert", "rows", None),
        P("expert", "rows"),
        P("expert", "rows"),
        P("expert", "rows"),
    )
    return jax.shard_map(
        shards,
        mesh=mesh,
        in_specs=placed,
        out_specs=(
            P("expert", "rows", None),
            P("expert", "rows"),
            P("expert", "rows"),
            P("expert", "rows"),
        ),
        check_vma=False,
    )
```

profile of v0, /device:TPU:14, one launch (start us, length us, event | category | flops | bytes accessed | tf_op | source)
XLA Modules:
  0.0 155.5 jit_solution(15498681350571910622)
XLA Ops:
  0.6 0.0 copy-start.2
  0.6 0.0 copy-start.1
  1.4 20.0 %fusion.1 = (f32[14336]{0:T(1024)S(1)}, f32[512]{0:T(512)S(1)}) fusion(bf16[1,512,14336]{2,1,0:T(8,128)(2,1)} %param.7), kind=kLoop, calls=%fused_computation.3 | loop fusion | flops 36685312 | bytes 14739456 | tf_op jit(solution)/shard_map/reduce_sum | solution.py:18
  21.4 0.0 copy-done.2
  21.4 0.6 fusion.4
  22.0 0.0 copy-start
  22.0 31.1 %all-reduce = (f32[1]{0:T(128)}, f32[1,14336]{1,0:T(1,128)S(1)}) all-reduce(f32[1]{0:T(128)} %bitcast.4, f32[1,14336]{1,0:T(1,128)S(1)} %bitcast.9), channel_id=1, replica_groups=mesh['expert'=4,'rows'=8] {'rows'}, use_global_device_ids=true, to_apply=%region_4.0 | all-reduce | flops 14337 | bytes 114696 | tf_op jit(solution)/shard_map/psum | solution.py:22
  53.1 0.0 copy-done.1
  53.1 30.4 %all_gather.3 = f32[1,14336]{1,0:T(1,128)S(1)} all-gather(f32[1,1792]{1,0:T(1,128)S(1)} %copy-done.1), channel_id=1, replica_groups=mesh['expert'=4,'rows'=8] {'rows'}, dimensions={1}, use_global_device_ids=true | all-gather | bytes 64512 | tf_op jit(solution)/shard_map/all_gather | solution.py:26
  83.5 0.1 multiply_add_fusion
  84.2 46.5 %psum.23 = f32[]{:T(128)} all-reduce(f32[]{:T(128)} %bitcast.6), channel_id=1, replica_groups=mesh['expert'=4,'rows'=8] {'expert','rows'}, use_global_device_ids=true, to_apply=%region_5.0 | all-reduce | flops 1 | bytes 8 | tf_op jit(solution)/shard_map/psum | solution.py:21
  131.4 21.7 %multiply_reduce_fusion = (f32[]{:T(128)}, bf16[1,512,14336]{2,1,0:T(8,128)(2,1)}) fusion(f32[]{:T(128)S(6)} %sqrt.7, f32[]{:T(128)} %bitcast.5, f32[14336]{0:T(1024)S(1)} %bitcast.8, f32[512]{0:T(512)S(1)} %bitcast.10, bf16[1,512,14336]{2,1,0:T(8,128)(2,1)} %param.7, bf16[1,512,14336]{2,1,0:T(8,128)(2,1)} %param.8), kind=kLoop, calls=%fused_computation.6 | loop fusion | flops 80740352 | bytes 44099596 | tf_op jit(solution)/shard_map/reduce_sum | solution.py:34
  153.1 0.0 copy-done
  153.8 0.6 constant_dynamic-slice_fusion
  (1 shorter events, 0.0 us)
Async XLA Ops:
  0.6 20.8 %copy-start.2 = (f32[1,512]{1,0:T(1,128)S(1)}, f32[1,512]{1,0:T(1,128)}, u32[]{:S(2)}) copy-start(f32[1,512]{1,0:T(1,128)} %param.9) | copy-start | bytes 6148
  0.6 52.5 %copy-start.1 = (f32[1,1792]{1,0:T(1,128)S(1)}, f32[1,1792]{1,0:T(1,128)}, u32[]{:S(2)}) copy-start(f32[1,1792]{1,0:T(1,128)} %param.10) | copy-start | bytes 21508
  22.0 131.1 %copy-start = (f32[1,512]{1,0:T(1,128)}, f32[1,512]{1,0:T(1,128)S(1)}, u32[]{:S(2)}) copy-start(f32[1,512]{1,0:T(1,128)S(1)} %get-tuple-element.9) | copy-start | bytes 6148
where the time goes:
time: 156 us; the launch traced here: 155 us
  blocking collectives  108 us (69%)
  other arithmetic  42.4 us (27%)
  between operations  4.52 us (3%)
    psum x1, blocking collectives, shards(): clip_total = lax.psum(clip_term, ('expert', 'rows'))  46.5 us
    psum x1, blocking collectives, shards(): row_totals = lax.psum(row_sum, 'rows')  31.1 us
    all_gather x1, blocking collectives, shards(): old_full = lax.all_gather(col_state, 'rows', axis=1, tiled=True)  30.4 us
    reduce_sum x1, other arithmetic, shards(): new_msq = jnp.mean(update * update, axis=(1, 2)).reshape(local_experts, 1)  21.7 us
    reduce_sum x1, other arithmetic, shards(): partial_cols = jnp.sum(squares, axis=1)  20 us

commit v1 on v0

--- a/solution.py
+++ b/solution.py
@@ -23,7 +23,7 @@
     entries = prev_msq.shape[0] * prev_msq.shape[1] * expert_devices * row_devices
     clip = jnp.sqrt(clip_total / entries)
     row_mean = row_totals / all_rows
-    old_full = lax.all_gather(col_state, "rows", axis=1, tiled=True)
+    old_full = jnp.concatenate(lax.all_gather(col_state, "rows"), axis=1)
     col_totals = lax.psum(partial_cols, "rows")
     full_cols = beta * old_full + (1.0 - beta) * col_totals / all_rows
     width = columns // row_devices

time: 156 us -> 156 us (level)
  no operation moved by 1% of the time
where the time goes in v1:
time: 156 us
  blocking collectives  108 us (69%)
  other arithmetic  42.4 us (27%)
  between operations  4.53 us (3%)
    psum x1, blocking collectives, shards(): clip_total = lax.psum(clip_term, ('expert', 'rows'))  46.5 us
    psum x1, blocking collectives, shards(): row_totals = lax.psum(row_sum, 'rows')  31.1 us
    all_gather x1, blocking collectives, shards(): old_full = jnp.concatenate(lax.all_gather(col_state, 'rows'), axis=1)  30.4 us
    reduce_sum x1, other arithmetic, shards(): new_msq = jnp.mean(update * update, axis=(1, 2)).reshape(local_experts, 1)  21.7 us
    reduce_sum x1, other arithmetic, shards(): partial_cols = jnp.sum(squares, axis=1)  20 us

profile of v1, /device:TPU:14, one launch (start us, length us, event | category | flops | bytes accessed | tf_op | source)
XLA Modules:
  0.0 155.5 jit_solution(936862337444378082)
XLA Ops:
  0.6 0.0 copy-start.2
  0.6 0.0 copy-start.1
  1.4 20.0 %fusion.1 = (f32[14336]{0:T(1024)S(1)}, f32[512]{0:T(512)S(1)}) fusion(bf16[1,512,14336]{2,1,0:T(8,128)(2,1)} %param.7), kind=kLoop, calls=%fused_computation.3 | loop fusion | flops 36685312 | bytes 14739456 | tf_op jit(solution)/shard_map/reduce_sum | solution.py:18
  21.4 0.0 copy-done.2
  21.4 0.6 fusion.4
  22.0 0.0 copy-start
  22.0 31.1 %all-reduce = (f32[1]{0:T(128)}, f32[1,14336]{1,0:T(1,128)S(1)}) all-reduce(f32[1]{0:T(128)} %bitcast.6, f32[1,14336]{1,0:T(1,128)S(1)} %bitcast.13), channel_id=1, replica_groups=mesh['expert'=4,'rows'=8] {'rows'}, use_global_device_ids=true, to_apply=%region_4.0 | all-reduce | flops 14337 | bytes 114696 | tf_op jit(solution)/shard_map/psum | solution.py:22
  53.1 0.0 copy-done.1
  53.1 30.4 %all-gather.1 = f32[8,1,1792]{2,1,0:T(1,128)S(1)} all-gather(f32[1,1,1792]{2,1,0:T(1,128)S(1)} %bitcast.18), channel_id=2, replica_groups=mesh['expert'=4,'rows'=8] {'rows'}, dimensions={0}, use_global_device_ids=true | all-gather | bytes 64512 | tf_op jit(solution)/shard_map/all_gather | solution.py:26
  83.5 0.1 multiply_add_fusion
  84.3 46.5 %psum.23 = f32[]{:T(128)} all-reduce(f32[]{:T(128)} %bitcast.8), channel_id=1, replica_groups=mesh['expert'=4,'rows'=8] {'expert','rows'}, use_global_device_ids=true, to_apply=%region_5.0 | all-reduce | flops 1 | bytes 8 | tf_op jit(solution)/shard_map/psum | solution.py:21
  131.4 21.7 %multiply_reduce_fusion = (f32[]{:T(128)}, bf16[1,512,14336]{2,1,0:T(8,128)(2,1)}) fusion(f32[]{:T(128)S(6)} %sqrt.7, f32[]{:T(128)} %bitcast.7, f32[14336]{0:T(1024)S(1)} %bitcast.12, f32[512]{0:T(512)S(1)} %bitcast.16, bf16[1,512,14336]{2,1,0:T(8,128)(2,1)} %param.7, bf16[1,512,14336]{2,1,0:T(8,128)(2,1)} %param.8), kind=kLoop, calls=%fused_computation.6 | loop fusion | flops 80740352 | bytes 44099596 | tf_op jit(solution)/shard_map/reduce_sum | solution.py:34
  153.1 0.0 copy-done
  153.8 0.6 constant_dynamic-slice_fusion
  (2 shorter events, 0.0 us)
Async XLA Ops:
  0.6 20.8 %copy-start.2 = (f32[1,512]{1,0:T(1,128)S(1)}, f32[1,512]{1,0:T(1,128)}, u32[]{:S(2)}) copy-start(f32[1,512]{1,0:T(1,128)} %param.9) | copy-start | bytes 6148
  0.6 52.5 %copy-start.1 = (f32[1,1792]{1,0:T(1,128)S(1)}, f32[1,1792]{1,0:T(1,128)}, u32[]{:S(2)}) copy-start(f32[1,1792]{1,0:T(1,128)} %param.10) | copy-start | bytes 21508
  22.0 131.1 %copy-start = (f32[1,512]{1,0:T(1,128)}, f32[1,512]{1,0:T(1,128)S(1)}, u32[]{:S(2)}) copy-start(f32[1,512]{1,0:T(1,128)S(1)} %get-tuple-element.9) | copy-start | bytes 6148

commit v2 on v0

--- a/solution.py
+++ b/solution.py
@@ -19,7 +19,11 @@
     clip_term = jnp.sum(prev_msq)
     row_sum = jnp.sum(new_row, axis=1)
     clip_total = lax.psum(clip_term, ("expert", "rows"))
-    row_totals = lax.psum(row_sum, "rows")
+    row_totals = row_sum
+    for hop in (1, 2, 4):
+        row_totals = row_totals + lax.ppermute(
+            row_totals, "rows", [(dev, dev ^ hop) for dev in range(8)]
+        )
     entries = prev_msq.shape[0] * prev_msq.shape[1] * expert_devices * row_devices
     clip = jnp.sqrt(clip_total / entries)
     row_mean = row_totals / all_rows

time: 156 us -> 167 us (1.071)
  waiting for transfers between devices: 0 us -> 5.25 us
  starting transfers between devices: 0 us -> 3.33 us
  between operations: 4.52 us -> 6.66 us
    ppermute x0 -> x3, waiting for transfers between devices: none -> 5.25 us  [shards(): lax.ppermute(row_totals, 'rows', [(dev, dev ^ hop) for dev in range(8)])]
    ppermute x0 -> x3, starting transfers between devices: none -> 3.33 us  [shards(): lax.ppermute(row_totals, 'rows', [(dev, dev ^ hop) for dev in range(8)])]
  transfers between devices with their start and end apart: 0 -> 3, of which waited for: 0 -> 2; matrix products, arithmetic and copies ran while one was open for 0% -> 0% of each run, Pallas kernels for 0% -> 0%
where the time goes in v2:
time: 167 us; the launch traced here: 166 us
  blocking collectives  108 us (65%)
  other arithmetic  42.5 us (25%)
  between operations  6.66 us (4%)
  waiting for transfers between devices  5.25 us (3%)
  starting transfers between devices  3.33 us (2%)
    psum x1, blocking collectives, shards(): clip_total = lax.psum(clip_term, ('expert', 'rows'))  46.4 us
    all_gather x1, blocking collectives, shards(): old_full = lax.all_gather(col_state, 'rows', axis=1, tiled=True)  30.8 us
    psum x1, blocking collectives, shards(): col_totals = lax.psum(partial_cols, 'rows')  30.8 us
    reduce_sum x1, other arithmetic, shards(): new_msq = jnp.mean(update * update, axis=(1, 2)).reshape(local_experts, 1)  21.8 us
    reduce_sum x1, other arithmetic, shards(): partial_cols = jnp.sum(squares, axis=1)  20 us
    ppermute x3, waiting for transfers between devices, shards(): lax.ppermute(row_totals, 'rows', [(dev, dev ^ hop) for dev in range(8)])  5.25 us
  transfers between devices with their start and end apart: 3, of which 2 were waited for; matrix products, arithmetic and copies ran while one was open for 0% of the time, Pallas kernels for 0%

profile of v2, /device:TPU:14, one launch (start us, length us, event | category | flops | bytes accessed | tf_op | source)
XLA Modules:
  0.0 166.3 jit_solution(4603503199658933721)
XLA Ops:
  0.6 0.0 copy-start.2
  0.6 0.0 copy-start.1
  1.4 20.0 %fusion.1 = (f32[14336]{0:T(1024)S(1)}, f32[512]{0:T(512)S(1)}) fusion(bf16[1,512,14336]{2,1,0:T(8,128)(2,1)} %param.7), kind=kLoop, calls=%fused_computation.3 | loop fusion | flops 36685312 | bytes 14739456 | tf_op jit(solution)/shard_map/reduce_sum | solution.py:18
  21.4 0.0 copy-done.2
  21.4 0.6 fusion.4
  22.0 0.0 copy-start
  22.0 0.5 collective-permute-start
  22.5 30.8 %psum.14 = f32[1,14336]{1,0:T(1,128)S(1)} all-reduce(f32[1,14336]{1,0:T(1,128)S(1)} %bitcast.9), channel_id=1, replica_groups=mesh['expert'=4,'rows'=8] {'rows'}, use_global_device_ids=true, to_apply=%region_2.0 | all-reduce | flops 14336 | bytes 114688 | tf_op jit(solution)/shard_map/psum | solution.py:31
  53.3 0.0 copy-done.1
  53.3 30.8 %all_gather.3 = f32[1,14336]{1,0:T(1,128)S(1)} all-gather(f32[1,1792]{1,0:T(1,128)S(1)} %copy-done.1), channel_id=1, replica_groups=mesh['expert'=4,'rows'=8] {'rows'}, dimensions={1}, use_global_device_ids=true | all-gather | bytes 64512 | tf_op jit(solution)/shard_map/all_gather | solution.py:30
  84.1 46.4 %psum.15 = f32[]{:T(128)} all-reduce(f32[]{:T(128)} %bitcast.6), channel_id=1, replica_groups=mesh['expert'=4,'rows'=8] {'expert','rows'}, use_global_device_ids=true, to_apply=%region_4.0 | all-reduce | flops 1 | bytes 8 | tf_op jit(solution)/shard_map/psum | solution.py:21
  131.2 0.1 multiply_add_fusion
  131.3 0.6 constant_dynamic-slice_fusion
  131.9 0.0 collective-permute-done
  133.2 1.4 collective-permute-start.1
  134.6 2.2 %collective-permute-done.1 = f32[1]{0:T(128)} collective-permute-done((f32[1]{0:T(128)}, f32[1]{0:T(128)}, u32[]{:S(2)}, u32[]{:S(2)}) %collective-permute-start.1) | collective-permute-done | bytes 36 | tf_op jit(solution)/shard_map/ppermute | solution.py:24
  137.5 1.5 collective-permute-start.2
  139.0 3.0 %collective-permute-done.2 = f32[1]{0:T(128)} collective-permute-done((f32[1]{0:T(128)}, f32[1]{0:T(128)}, u32[]{:S(2)}, u32[]{:S(2)}) %collective-permute-start.2) | collective-permute-done | bytes 36 | tf_op jit(solution)/shard_map/ppermute | solution.py:24
  142.7 21.8 %multiply_reduce_fusion = (f32[]{:T(128)}, bf16[1,512,14336]{2,1,0:T(8,128)(2,1)}) fusion(f32[]{:T(128)S(6)} %sqrt.7, f32[]{:T(128)} %bitcast.5, f32[14336]{0:T(1024)S(1)} %bitcast.8, f32[512]{0:T(512)S(1)} %bitcast.10, bf16[1,512,14336]{2,1,0:T(8,128)(2,1)} %param.7, bf16[1,512,14336]{2,1,0:T(8,128)(2,1)} %param.8), kind=kLoop, calls=%fused_computation.6 | loop fusion | flops 80740352 | bytes 44099596 | tf_op jit(solution)/shard_map/reduce_sum | solution.py:38
  164.5 0.0 copy-done
  (1 shorter events, 0.0 us)
Async XLA Ops:
  0.6 20.8 %copy-start.2 = (f32[1,512]{1,0:T(1,128)S(1)}, f32[1,512]{1,0:T(1,128)}, u32[]{:S(2)}) copy-start(f32[1,512]{1,0:T(1,128)} %param.9) | copy-start | bytes 6148
  0.6 52.6 %copy-start.1 = (f32[1,1792]{1,0:T(1,128)S(1)}, f32[1,1792]{1,0:T(1,128)}, u32[]{:S(2)}) copy-start(f32[1,1792]{1,0:T(1,128)} %param.10) | copy-start | bytes 21508
  22.0 142.4 %copy-start = (f32[1,512]{1,0:T(1,128)}, f32[1,512]{1,0:T(1,128)S(1)}, u32[]{:S(2)}) copy-start(f32[1,512]{1,0:T(1,128)S(1)} %get-tuple-element.7) | copy-start | bytes 6148
  22.0 109.9 %collective-permute-start = (f32[1]{0:T(128)}, f32[1]{0:T(128)}, u32[]{:S(2)}, u32[]{:S(2)}) collective-permute-start(f32[1]{0:T(128)} %bitcast.4), channel_id=1, source_target_pairs={{0,1},{1,0},{2,3},{3,2},{4,5},{5,4},{6,7},{7,6},{8,9},{9,8},{10,11... | collective-permute-start | bytes 20 | tf_op jit(solution)/shard_map/ppermute | solution.py:24
  133.2 3.6 %collective-permute-start.1 = (f32[1]{0:T(128)}, f32[1]{0:T(128)}, u32[]{:S(2)}, u32[]{:S(2)}) collective-permute-start(f32[1]{0:T(128)} %add.35), channel_id=1, source_target_pairs={{0,2},{1,3},{2,0},{3,1},{4,6},{5,7},{6,4},{7,5},{8,10},{9,11},{10,... | collective-permute-start | bytes 20 | tf_op jit(solution)/shard_map/ppermute | solution.py:24
  137.5 4.5 %collective-permute-start.2 = (f32[1]{0:T(128)}, f32[1]{0:T(128)}, u32[]{:S(2)}, u32[]{:S(2)}) collective-permute-start(f32[1]{0:T(128)} %add.36), channel_id=1, source_target_pairs={{0,4},{1,5},{2,6},{3,7},{4,0},{5,1},{6,2},{7,3},{8,12},{9,13},{10,... | collective-permute-start | bytes 20 | tf_op jit(solution)/shard_map/ppermute | solution.py:24
